TPU v7x, 32 devices: a whole 2x2x4 slice. The times are simulated.
32 devices in a mesh: seq: 16 (over z, y, x), tp: 2 (over core).
Axes of the slice: x: 2, y: 2, z: 4, core: 2. Of those that a mesh axis runs over, the one named last changes fastest.
Arguments:
- latent: bfloat16 [2, 16, 256, 1152], P(None, 'seq', 'tp'), may hold values from -6 to 6
- modulation: float32 [2, 9, 1152], replicated, may hold values from -4 to 4
- qkv_spatial: bfloat16 [3, 1152, 1152], P(None, None, 'tp'), may hold values from -0.1875 to 0.1875
- gain_spatial: float32 [2, 72], replicated, may hold values from 0.5 to 1.7
- out_spatial: bfloat16 [1152, 1152], P('tp'), may hold values from -0.1875 to 0.1875
- qkv_temporal: bfloat16 [3, 1152, 1152], P(None, None, 'tp'), may hold values from -0.1875 to 0.1875
- gain_temporal: float32 [2, 72], replicated, may hold values from 0.5 to 1.7
- out_temporal: bfloat16 [1152, 1152], P('tp'), may hold values from -0.1875 to 0.1875
- fc_in: bfloat16 [1152, 4608], P(None, 'tp'), may hold values from -0.1875 to 0.1875
- fc_out: bfloat16 [4608, 1152], P('tp'), may hold values from -0.09375 to 0.09375
Outputs:
- result: bfloat16 [2, 16, 256, 1152], P(None, 'seq', 'tp')
All inputs are finite; a program needn't handle non-finite values.
Results may differ from a plain program's by a relative error of at most 0.017.
Values may be sent and summed in bfloat16 or wider, within the bound.
A program may use at most 64 MiB of HBM per device.

v0:
```python
import math

import jax
import jax.numpy as jnp
from jax import lax
from jax.sharding import PartitionSpec as P

D = 1152
H = 16


epsilon = 1e-06


def layer_norm(values):
    average = jnp.mean(values, axis=-1, keepdims=True)
    centred = values - average
    variance = jnp.mean(centred * centred, axis=-1, keepdims=True)
    return centred * lax.rsqrt(variance + epsilon)


def modulated(field, modulation, offset):
    shift_row = modulation[:, offset][:, None, None, :]
    scale_row = modulation[:, offset + 1][:, None, None, :]
    return (layer_norm(field) * (1.0 + scale_row) + shift_row).astype(jnp.bfloat16)


def project_heads(rows_piece, table, gains, head_dim):
    results = []
    for which_part in range(3):
        projected = jnp.einsum(
            "bfpd,de->bfpe", rows_piece, table[which_part], preferred_element_type=jnp.float32
        )
        if which_part < 2:
            shaped = projected.reshape(
                projected.shape[:-1] + (projected.shape[-1] // head_dim, head_dim)
            )
            shaped = (
                shaped
                * lax.rsqrt(jnp.mean(shaped * shaped, axis=-1, keepdims=True) + epsilon)
                * gains[which_part]
            )
            projected = shaped.reshape(projected.shape)
        results.append(projected.astype(jnp.bfloat16))
    return jnp.stack(results)


def attend(query_rows, key_rows, value_rows, head_dim):
    groups, length, feature_width = query_rows.shape
    head_count = feature_width // head_dim
    query_heads = query_rows.reshape(groups, length, head_count, head_dim)
    key_heads = key_rows.reshape(groups, length, head_count, head_dim)
    value_heads = value_rows.reshape(groups, length, head_count, head_dim)
    block_rows = min(length, 512)

    def one_block(first_row):
        query_block = lax.dynamic_slice_in_dim(query_heads, first_row, block_rows, 1)
        scores = jnp.einsum(
            "gqhe,gkhe->ghqk", query_block, key_heads, preferred_element_type=jnp.float32
        ) / math.sqrt(head_dim)
        weights = jnp.exp(scores)
        probabilities = (weights / jnp.sum(weights, axis=-1, keepdims=True)).astype(jnp.bfloat16)
        return jnp.einsum(
            "ghqk,gkhe->gqhe", probabilities, value_heads, preferred_element_type=jnp.float32
        ).astype(jnp.bfloat16)

    starts = jnp.arange(length // block_rows, dtype=jnp.int32) * block_rows
    pieces = lax.map(one_block, starts)
    return pieces.transpose(1, 0, 2, 3, 4).reshape(groups, length, feature_width)


def frame_attention(query_rows, key_rows, value_rows, head_dim):
    batches, frames, patches, feature_width = query_rows.shape
    members = [
        item.transpose(0, 2, 1, 3).reshape(batches * patches, frames, feature_width)
        for item in (query_rows, key_rows, value_rows)
    ]
    mixed_heads = attend(members[0], members[1], members[2], head_dim)
    return mixed_heads.reshape(batches, patches, frames, feature_width).transpose(0, 2, 1, 3)


def body(
    latent,
    modulation,
    qkv_spatial,
    gain_spatial,
    out_spatial,
    qkv_temporal,
    gain_temporal,
    out_temporal,
    fc_in,
    fc_out,
):
    head_dim = D // H
    running = latent.astype(jnp.float32)
    normed = modulated(running, modulation, 0)
    packed = project_heads(
        lax.all_gather(normed, "tp", axis=2, tiled=True), qkv_spatial, gain_spatial, head_dim
    )
    batches, frames, patches, local_width = packed.shape[1:]
    mixed_heads = attend(
        packed[0].reshape(batches * frames, patches, local_width),
        packed[1].reshape(batches * frames, patches, local_width),
        packed[2].reshape(batches * frames, patches, local_width),
        head_dim,
    )
    mixed_heads = mixed_heads.reshape(batches, frames, patches, local_width)
    partial_value = jnp.einsum(
        "bfpe,ed->bfpd", mixed_heads, out_spatial, preferred_element_type=jnp.float32
    )
    spatial_out = lax.psum_scatter(
        partial_value.astype(jnp.bfloat16), "tp", scatter_dimension=2, tiled=True
    )
    running = running + modulation[:, 2][:, None, None, :] * spatial_out.astype(jnp.float32)
    normed = modulated(running, modulation, 3)
    moved_rows = lax.all_to_all(normed, "seq", split_axis=2, concat_axis=1, tiled=True)
    packed = project_heads(
        lax.all_gather(moved_rows, "tp", axis=2, tiled=True), qkv_temporal, gain_temporal, head_dim
    )
    mixed_heads = frame_attention(packed[0], packed[1], packed[2], head_dim)
    partial_value = jnp.einsum(
        "bfpe,ed->bfpd", mixed_heads, out_temporal, preferred_element_type=jnp.float32
    )
    shares = lax.psum_scatter(
        partial_value.astype(jnp.bfloat16), "tp", scatter_dimension=2, tiled=True
    )
    temporal_out = lax.all_to_all(shares, "seq", split_axis=1, concat_axis=2, tiled=True)
    running = running + modulation[:, 5][:, None, None, :] * temporal_out.astype(jnp.float32)
    normed = modulated(running, modulation, 6)
    projected = jnp.einsum(
        "bfpd,de->bfpe",
        lax.all_gather(normed, "tp", axis=2, tiled=True),
        fc_in,
        preferred_element_type=jnp.float32,
    )
    hidden = jax.nn.gelu(projected, approximate=True).astype(jnp.bfloat16)
    partial_value = jnp.einsum("bfpe,ed->bfpd", hidden, fc_out, preferred_element_type=jnp.float32)
    mlp_out = lax.psum_scatter(
        partial_value.astype(jnp.bfloat16), "tp", scatter_dimension=2, tiled=True
    )
    return (running + modulation[:, 8][:, None, None, :] * mlp_out.astype(jnp.float32)).astype(
        jnp.bfloat16
    )


def solution(mesh):
    placed = (
        P(None, "seq", "tp", None),
        P(),
        P(None, None, "tp"),
        P(),
        P("tp", None),
        P(None, None, "tp"),
        P(),
        P("tp", None),
        P(None, "tp"),
        P("tp", None),
    )
    return jax.shard_map(
        body, mesh=mesh, in_specs=placed, out_specs=P(None, "seq", "tp", None), check_vma=False
    )
```

profile of v0, /device:TPU:29, one launch (start us, length us, event | category | flops | bytes accessed | tf_op | source)
XLA Modules:
  0.0 188.4 jit_solution(2807091613973936271)
XLA Ops:
  6.5 1.0 slice_bitcast_fusion.1
  7.5 1.2 convert_reduce_fusion
  8.7 1.4 fusion.49
  10.1 1.1 fusion.52
  11.5 10.8 %all-gather.4.cloned.1.call-done = bf16[2,1,256,1152]{3,2,0,1:T(8,128)(2,1)} async-done(((bf16[2,1,128,1152]{3,2,0,1:T(8,128)(2,1)}), bf16[2,1,256,1152]{3,2,0,1:T(8,128)(2,1)}) %all-gather.4.cloned.1.call-update) | async-done | bytes 1179664 | tf_op jit(solution)/shard_map/all_gather | solution.py:98
  22.3 3.7 %fusion.88 = (f32[2,256,576]{1,2,0:T(8,128)}, f32[2,256,576]{1,2,0:T(8,128)S(1)}) fusion(bf16[3,1152,576]{1,2,0:T(8,128)(2,1)} %param.12, bf16[2,1,256,1152]{3,2,0,1:T(8,128)(2,1)} %all-gather.4.cloned.1.call-done), kind=kOutput, calls=%fused_computation.119 | convolution fusion | flops 679772160 | bytes 4866048 | tf_op jit(solution)/shard_map/bfpd,de->bfpe/dot_general | solution.py:31
  26.0 1.4 reduce_sum.113
  27.4 4.1 %fusion.87 = (f32[2,256,576]{1,2,0:T(8,128)}, f32[2,256,576]{1,2,0:T(8,128)}) fusion(bf16[3,1152,576]{1,2,0:T(8,128)(2,1)} %param.12, bf16[2,1,256,1152]{3,2,0,1:T(8,128)(2,1)} %all-gather.4.cloned.1.call-done), kind=kOutput, calls=%fused_computation.118 | convolution fusion | flops 679772160 | bytes 4866048 | tf_op jit(solution)/shard_map/bfpd,de->bfpe/dot_general | solution.py:31
  31.4 1.4 reduce_sum.112
  33.0 1.0 copy-done.4
  34.3 0.9 fusion.16
  35.2 0.3 copy-done.5
  35.6 2.3 %fusion.43 = bf16[2,256,576]{1,2,0:T(8,128)(2,1)S(1)} fusion(bf16[3,1152,576]{1,2,0:T(8,128)(2,1)} %param.12, bf16[2,1,256,1152]{3,2,0,1:T(8,128)(2,1)S(1)} %copy-done.5), kind=kOutput, calls=%fused_computation.51 | convolution fusion | flops 679772160 | bytes 3096576 | tf_op jit(solution)/shard_map/bfpd,de->bfpe/dot_general | solution.py:31
  37.8 0.9 fusion.42
  38.7 2.2 %fusion.20 = bf16[2,1,256,1152]{3,2,0,1:T(8,128)(2,1)} fusion(bf16[2,256,576]{1,2,0:T(8,128)(2,1)S(1)} %bitcast.217, bf16[576,1152]{1,0:T(8,128)(2,1)S(1)} %copy-done), kind=kOutput, calls=%fused_computation.19 | convolution fusion | flops 680067072 | bytes 3096576 | tf_op jit(solution)/shard_map/bfpe,ed->bfpd/dot_general | solution.py:108
  41.0 9.8 %reduce-scatter.6.cloned.1.call-done = bf16[2,1,128,1152]{3,2,0,1:T(8,128)(2,1)} async-done(((bf16[2,1,256,1152]{3,2,0,1:T(8,128)(2,1)}), bf16[2,1,128,1152]{3,2,0,1:T(8,128)(2,1)}) %reduce-scatter.6.cloned.1.call-update) | async-done | bytes 589840 | tf_op jit(solution)/shard_map/reduce_scatter | solution.py:111
  50.8 1.4 fusion.75
  52.2 0.4 multiply_reduce_fusion.3
  52.6 0.4 add_convert_fusion.2
  53.0 0.6 copy.31
  53.6 20.9 %all_to_all.21 = bf16[2,1,128,1152]{3,0,1,2:T(2,128)(2,1)S(1)} all-to-all(bf16[2,1,128,1152]{3,0,1,2:T(2,128)(2,1)S(1)} %copy.31), channel_id=1, replica_groups=mesh['seq'=16,'tp'=2] {'seq'}, dimensions={2} | all-to-all | bytes 1179648 | tf_op jit(solution)/shard_map/all_to_all | solution.py:116
  74.5 0.9 copy.76
  75.4 3.0 %fusion.86 = (bf16[1,1152,576]{1,2,0:T(8,128)(2,1)S(1)}, bf16[1,1152,576]{1,2,0:T(8,128)(2,1)}) fusion(bf16[3,1152,576]{1,2,0:T(8,128)(2,1)} %param.15), kind=kLoop, calls=%fused_computation.117 | loop fusion | bytes 5308416 | tf_op jit(solution)/shard_map/slice | solution.py:32
  78.5 7.2 %all-gather.6.cloned.1.call-done = bf16[2,16,16,1152]{3,2,1,0:T(8,128)(2,1)} async-done(((bf16[2,16,8,1152]{3,2,1,0:T(8,128)(2,1)}), bf16[2,16,16,1152]{3,2,1,0:T(8,128)(2,1)}) %all-gather.6.cloned.1.call-update) | async-done | bytes 1179664 | tf_op jit(solution)/shard_map/all_gather | solution.py:118
  85.7 3.5 %multiply_reduce_fusion = (f32[2,16,16,8]{2,3,1,0:T(8,128)S(1)}, f32[2,16,16,8,72]{4,2,3,1,0:T(8,128)S(1)}) fusion(bf16[8,72,1152,1,1]{2,1,0,4,3:T(8,128)(2,1)} %bitcast.212, bf16[2,16,16,1152]{3,2,1,0:T(8,128)(2,1)} %all-gather.6.cloned.1.call-done), kind=kOutput, calls=%fused_computation.24 | convolution fusion | flops 680062976 | bytes 3702784 | tf_op jit(solution)/shard_map/bfpd,de->bfpe/dot_general | solution.py:31
  89.3 1.8 multiply_reduce_fusion.1
  91.1 2.3 %multiply_convert_fusion = (bf16[2,16,16,8,72]{4,2,3,1,0:T(8,128)(2,1)}, bf16[2,16,16,8,72]{4,2,3,1,0:T(8,128)(2,1)S(1)}) fusion(f32[2,16,16,8,72]{4,2,3,1,0:T(8,128)S(1)} %get-tuple-element.59, f32[72]{0:T(128)S(1)} %get-tuple-element.49, f32[2,16,16,8]{2,3,1,0:T(8,128)S(1)} %add_rsqrt_fusion, f32[72]{0:T(128)S(1)} %get-tuple-element.48, ...), kind=kLoop, calls=%fused_computation.23 | loop fusion | flops 1769472 | bytes 3572288 | tf_op jit(solution)/shard_map/convert_element_type | solution.py:44
  93.7 0.8 convert_element_type.122
  94.6 2.0 %reshape_reshape.10 = bf16[32,16,8,72]{3,2,1,0:T(8,128)(2,1)} reshape(bf16[2,16,16,576]{3,2,1,0:T(8,128)(2,1)S(1)} %copy.35) | data formatting | bytes 1179648 | tf_op jit(solution)/shard_map/reshape;reshape | solution.py:51
  96.7 1.5 copy.36
  98.2 0.8 convert_element_type.124
  99.1 2.0 %reshape_reshape.11 = bf16[32,16,8,72]{3,2,1,0:T(8,128)(2,1)} reshape(bf16[2,16,16,576]{3,2,1,0:T(8,128)(2,1)S(1)} %copy.37) | data formatting | bytes 1179648 | tf_op jit(solution)/shard_map/reshape;reshape | solution.py:52
  101.1 2.9 %fusion.46 = bf16[2,16,16,576]{3,1,2,0:T(8,128)(2,1)S(1)} fusion(bf16[2,16,16,1152]{3,2,1,0:T(8,128)(2,1)} %all-gather.6.cloned.1.call-done, bf16[3,1152,576]{1,2,0:T(8,128)(2,1)} %param.15), kind=kOutput, calls=%fused_computation.52 | convolution fusion | flops 679772160 | bytes 3096576 | tf_op jit(solution)/shard_map/bfpd,de->bfpe/dot_general | solution.py:31
  104.1 2.0 %reshape_reshape.9 = bf16[32,16,8,72]{3,2,1,0:T(8,128)(2,1)} reshape(bf16[2,16,16,576]{3,2,1,0:T(8,128)(2,1)S(1)} %copy.33) | data formatting | bytes 1179648 | tf_op jit(solution)/shard_map/reshape;reshape | solution.py:53
  106.1 2.2 %fusion.25 = (f32[32,8,16]{2,1,0:T(8,128)S(1)}, f32[32,8,16,16]{2,3,1,0:T(8,128)S(1)}) fusion(bf16[32,16,8,72]{3,2,1,0:T(8,128)(2,1)} %reshape_reshape.11, bf16[32,16,8,72]{3,2,1,0:T(8,128)(2,1)S(1)} %copy-done.6), kind=kOutput, calls=%fused_computation.28 | convolution fusion | flops 9564160 | bytes 1458176 | tf_op jit(solution)/shard_map/while/body/eval_jaxpr/gqhe,gkhe->ghqk/dot_general | solution.py:58
  108.3 0.7 fusion.28
  109.3 0.8 reshape_reshape_transpose.4
  110.1 2.5 %convolution_convert_fusion = bf16[2,16,16,1152]{3,2,1,0:T(8,128)(2,1)S(1)} fusion(bf16[576,1152]{1,0:T(8,128)(2,1)} %param.17, bf16[2,16,16,576]{3,1,2,0:T(8,128)(2,1)S(1)} %bitcast.214), kind=kOutput, calls=%fused_computation.17 | convolution fusion | flops 680067072 | bytes 3096576 | tf_op jit(solution)/shard_map/bfpe,ed->bfpd/dot_general | solution.py:121
  112.6 1.1 copy.57
  113.8 9.8 %reduce-scatter.10.cloned.1.call-done = bf16[8,36864]{1,0:T(8,128)(2,1)} async-done(((bf16[16,36864]{1,0:T(8,128)(2,1)}), bf16[8,36864]{1,0:T(8,128)(2,1)}) %reduce-scatter.10.cloned.1.call-update) | async-done | bytes 589840
  123.6 1.1 copy.44
  124.7 20.9 %all_to_all.22 = bf16[2,16,8,1152]{3,2,0,1:T(8,128)(2,1)S(1)} all-to-all(bf16[2,16,8,1152]{3,2,0,1:T(8,128)(2,1)S(1)} %copy.44), channel_id=1, replica_groups=mesh['seq'=16,'tp'=2] {'seq'}, dimensions={1} | all-to-all | bytes 1179648 | tf_op jit(solution)/shard_map/all_to_all | solution.py:127
  145.5 0.4 fusion.84
  146.2 1.1 add_convert_fusion.1
  147.6 10.1 %all-gather.8.cloned.1.call-done = bf16[2,1,256,1152]{3,2,0,1:T(8,128)(2,1)} async-done(((bf16[2,1,128,1152]{3,2,0,1:T(8,128)(2,1)}), bf16[2,1,256,1152]{3,2,0,1:T(8,128)(2,1)}) %all-gather.8.cloned.1.call-update) | async-done | bytes 1179664 | tf_op jit(solution)/shard_map/all_gather | solution.py:132
  157.7 11.9 %fusion.21 = bf16[2,1,256,1152]{3,2,0,1:T(8,128)(2,1)} fusion(bf16[2304,1152]{1,0:T(8,128)(2,1)} %param.19, bf16[1152,2304]{1,0:T(8,128)(2,1)} %param.18, bf16[2,1,256,1152]{3,2,0,1:T(8,128)(2,1)} %all-gather.8.cloned.1.call-done), kind=kOutput, calls=%fused_computation.20 | convolution fusion | flops 5447024640 | bytes 12976128 | tf_op jit(solution)/shard_map/bfpe,ed->bfpd/dot_general | solution.py:137
  169.6 9.8 %reduce-scatter.8.cloned.1.call-done = bf16[2,1,128,1152]{3,2,0,1:T(8,128)(2,1)} async-done(((bf16[2,1,256,1152]{3,2,0,1:T(8,128)(2,1)}), bf16[2,1,128,1152]{3,2,0,1:T(8,128)(2,1)}) %reduce-scatter.8.cloned.1.call-update) | async-done | bytes 589840 | tf_op jit(solution)/shard_map/reduce_scatter | solution.py:138
  179.5 2.1 %fusion.77 = bf16[2,1,128,1152]{3,2,1,0:T(8,128)(2,1)} fusion(f32[2,1,128,1152]{3,2,0,1:T(8,128)S(1)} %get-tuple-element.24, bf16[2,1,128,1152]{3,2,0,1:T(8,128)(2,1)} %reduce-scatter.8.cloned.1.call-done, f32[2,1152]{1,0:T(2,128)S(1)} %get-tuple-element.32), kind=kLoop, calls=%fused_computation.85 | loop fusion | flops 1179648 | bytes 2368512 | tf_op jit(solution)/shard_map/convert_element_type | solution.py:141
  (56 shorter events, 2.4 us)
Async XLA Ops:
  6.5 32.2 %copy-start = (bf16[576,1152]{1,0:T(8,128)(2,1)S(1)}, bf16[576,1152]{1,0:T(8,128)(2,1)}, u32[]{:S(2)}) copy-start(bf16[576,1152]{1,0:T(8,128)(2,1)} %param.14) | copy-start | bytes 3981316
  6.5 3.6 %copy-start.2 = (bf16[2,1,128,1152]{3,2,1,0:T(8,128)(2,1)S(1)}, bf16[2,1,128,1152]{3,2,1,0:T(8,128)(2,1)}, u32[]{:S(2)}) copy-start(bf16[2,1,128,1152]{3,2,1,0:T(8,128)(2,1)} %param.10) | copy-start | bytes 1769476
  6.5 15.8 %all-gather.4.cloned.1.call-start = ((), (), s32[]{:S(2)}) async-start(), calls=%async_computation.5 | async-start | bytes 1769472 | tf_op jit(solution)/shard_map/all_gather | solution.py:98
  8.7 2.6 %copy-start.8 = (f32[2,72]{1,0:T(2,128)S(1)}, f32[2,72]{1,0:T(2,128)}, u32[]{:S(2)}) copy-start(f32[2,72]{1,0:T(2,128)} %param.13) | copy-start | bytes 1732
  11.3 39.5 %reduce-scatter.6.cloned.1.call-start = ((), (), s32[]{:S(2)}) async-start(), calls=%async_computation.6 | async-start | bytes 1769472 | tf_op jit(solution)/shard_map/reduce_scatter | solution.py:111
  32.8 1.3 copy-start.4
  34.3 1.3 copy-start.5
  41.0 44.8 %all-gather.6.cloned.1.call-start = ((), (), s32[]{:S(2)}) async-start(), calls=%async_computation.7 | async-start | bytes 1769472 | tf_op jit(solution)/shard_map/all_gather | solution.py:118
  50.8 1.4 copy-start.3
  74.5 1.0 copy-start.9
  75.4 48.2 %reduce-scatter.10.cloned.1.call-start = ((), (), s32[]{:S(2)}) async-start(), calls=%async_computation.10 | async-start | bytes 1769472
  85.7 3.6 %copy-start.10 = (bf16[2,16,16,1152]{3,2,1,0:T(8,128)(2,1)S(1)}, bf16[2,16,16,1152]{3,2,1,0:T(8,128)(2,1)}, u32[]{:S(2)}) copy-start(bf16[2,16,16,1152]{3,2,1,0:T(8,128)(2,1)} %all-gather.6.cloned.1.call-done) | copy-start | bytes 3538948
  104.1 2.0 %copy-start.6 = (bf16[32,16,8,72]{3,2,1,0:T(8,128)(2,1)S(1)}, bf16[32,16,8,72]{3,2,1,0:T(8,128)(2,1)}, u32[]{:S(2)}) copy-start(bf16[32,16,8,72]{3,2,1,0:T(8,128)(2,1)} %reshape_reshape.10) | copy-start | bytes 1769476
  106.1 2.2 %copy-start.7 = (bf16[32,16,8,72]{3,2,1,0:T(8,128)(2,1)S(1)}, bf16[32,16,8,72]{3,2,1,0:T(8,128)(2,1)}, u32[]{:S(2)}) copy-start(bf16[32,16,8,72]{3,2,1,0:T(8,128)(2,1)} %reshape_reshape.9) | copy-start | bytes 1769476
  113.7 44.0 %all-gather.8.cloned.1.call-start = ((), (), s32[]{:S(2)}) async-start(), calls=%async_computation.8 | async-start | bytes 1769472 | tf_op jit(solution)/shard_map/all_gather | solution.py:132
  147.4 32.1 %reduce-scatter.8.cloned.1.call-start = ((), (), s32[]{:S(2)}) async-start(), calls=%async_computation.9 | async-start | bytes 1769472 | tf_op jit(solution)/shard_map/reduce_scatter | solution.py:138
  179.5 2.1 %copy-start.1 = (bf16[576,1152]{1,0:T(8,128)(2,1)S(1)}, bf16[576,1152]{1,0:T(8,128)(2,1)}, u32[]{:S(2)}) copy-start(bf16[576,1152]{1,0:T(8,128)(2,1)} %param.14) | copy-start | bytes 3981316
Sparse Core Ops, SparseCore 0:
  11.4 10.8 all-gather.3
  41.1 9.6 reduce-scatter.5
  75.5 10.1 all-gather.5
  113.9 9.6 reduce-scatter.9
  147.5 10.1 all-gather.7
  169.8 9.6 reduce-scatter.7
where the time goes:
time: 190 us; the launch traced here: 188 us
  waiting for transfers between devices  57.6 us (30%)
  blocking collectives  41.8 us (22%)
  matrix products  39.4 us (21%)
  local copies, waits for them, and re-layouts  19.2 us (10%)
  other arithmetic  16.3 us (9%)
  between operations  13.8 us (7%)
    all_gather x2, waiting for transfers between devices, body(): lax.all_gather(normed, 'tp', axis=2, tiled=True)  20.9 us
    all_to_all x1, blocking collectives, body(): lax.all_to_all(normed, 'seq', split_axis=2, concat_axis=1, tiled=True)  20.9 us
    all_to_all x1, blocking collectives, body(): lax.all_to_all(shares, 'seq', split_axis=1, concat_axis=2, tiled=True)  20.9 us
    reduce_scatter x2, waiting for transfers between devices, body(): lax.psum_scatter(partial_value.astype(jnp.bfloat16), 'tp', scatter_dimens...  19.6 us
    dot_general x6, matrix products, project_heads(): jnp.einsum('bfpd,de->bfpe', rows_piece, table[which_part], preferred_elem...  18.2 us
    dot_general x1, matrix products, body(): jnp.einsum('bfpe,ed->bfpd', hidden, fc_out, preferred_element_type=jnp.fl...  11.9 us
    unnamed x7, waiting for transfers between devices  9.87 us
    all_gather x1, waiting for transfers between devices, body(): lax.all_gather(moved_rows, 'tp', axis=2, tiled=True)  7.24 us
  transfers between devices with their start and end apart: 6, of which 6 were waited for; matrix products, arithmetic and copies ran while one was open for 2% of the time, Pallas kernels for 0%

commit v1 on v0

--- a/solution.py
+++ b/solution.py
@@ -1,22 +1,303 @@
+import functools
 import math
 
 import jax
 import jax.numpy as jnp
 from jax import lax
+from jax.experimental import pallas as pl
+from jax.experimental.pallas import tpu as pltpu
 from jax.sharding import PartitionSpec as P
 
-D = 1152
-H = 16
-
-
-epsilon = 1e-06
+MESH = pl.DeviceIdType.MESH
+EPSILON = 1e-06
+BF16 = jnp.bfloat16
+F32 = jnp.float32
+
+
+def modnorm(rows, mod_ref, b, offset):
+    shift = mod_ref[b, offset : offset + 1, :]
+    scale = mod_ref[b, offset + 1 : offset + 2, :]
+    average = jnp.mean(rows, axis=-1, keepdims=True)
+    centred = rows - average
+    variance = jnp.mean(centred * centred, axis=-1, keepdims=True)
+    return centred * lax.rsqrt(variance + EPSILON) * (1.0 + scale) + shift
+
+
+def project(rows, table_ref, gain_ref, gain_row, same_head, head_dim):
+    results = []
+    for part in range(3):
+        y = jnp.dot(rows, table_ref[part], preferred_element_type=F32)
+        if part < 2:
+            squares = jnp.dot((y * y).astype(BF16), same_head, preferred_element_type=F32)
+            inverse = lax.rsqrt(squares * (1.0 / head_dim) + EPSILON)
+            y = y * inverse * gain_ref[gain_row + part : gain_row + part + 1, :]
+        results.append(y.astype(BF16))
+    return results
+
+
+def attend(query, key, value, heads_ref, head_dim, group):
+    length, width = query.shape
+    factor = math.log2(math.e) / math.sqrt(head_dim)
+    if group is not None:
+        row = lax.broadcasted_iota(jnp.int32, (length, length), 0)
+        column = lax.broadcasted_iota(jnp.int32, (length, length), 1)
+        same = lax.rem(row, group) == lax.rem(column, group)
+    heads_ref[...] = jnp.zeros_like(heads_ref)
+    for head in range(width // head_dim):
+        first, last = head * head_dim, (head + 1) * head_dim
+        low = first // 128 * 128
+        high = min((last + 127) // 128 * 128, width)
+        lane = lax.broadcasted_iota(jnp.int32, (1, high - low), 1) + low
+        mask = jnp.where((lane >= first) & (lane < last), 1.0, 0.0).astype(BF16)
+        scores = lax.dot_general(
+            query[:, low:high] * mask,
+            key[:, low:high],
+            (((1,), (1,)), ((), ())),
+            preferred_element_type=F32,
+        )
+        weights = jnp.exp2(scores * factor)
+        if group is not None:
+            weights = jnp.where(same, weights, 0.0)
+        total = jnp.sum(weights, axis=-1, keepdims=True)
+        probabilities = (weights * (1.0 / total)).astype(BF16)
+        heads_ref[:, low:high] += jnp.dot(
+            probabilities, value[:, low:high] * mask, preferred_element_type=F32
+        )
+    return heads_ref[...].astype(BF16)
+
+
+def gelu(u):
+    return 0.5 * u * (1.0 + jnp.tanh(math.sqrt(2.0 / math.pi) * (u + 0.044715 * (u * u * u))))
+
+
+def kernel(
+    n,
+    head_dim,
+    lat,
+    mod,
+    gains,
+    same_head_ref,
+    h_qkv_s,
+    h_out_s,
+    h_qkv_t,
+    h_out_t,
+    h_in,
+    h_out,
+    result,
+    qkv_s,
+    out_s,
+    qkv_t,
+    out_t,
+    w_in,
+    w_out,
+    lat_peer,
+    part,
+    got_s,
+    running,
+    mixed_f32,
+    send,
+    tokens,
+    got_t,
+    back_send,
+    back,
+    normed,
+    normed_peer,
+    hidden,
+    got_m,
+    heads,
+    w_sem,
+    pair_send,
+    pair_recv,
+    a_send,
+    a_recv,
+    f_send,
+    f_recv,
+    b_send,
+    b_recv,
+    own_sem,
+):
+    me = lax.axis_index("seq")
+    other = 1 - lax.axis_index("tp")
+    batches, patches, _ = lat.shape
+    block = batches * patches // n
+    small = patches // n
+
+    loads = [
+        pltpu.make_async_copy(source, target, w_sem.at[i])
+        for i, (source, target) in enumerate(
+            (
+                (h_qkv_s, qkv_s),
+                (h_out_s, out_s),
+                (h_qkv_t, qkv_t),
+                (h_out_t, out_t),
+                (h_in, w_in),
+                (h_out, w_out),
+            )
+        )
+    ]
+    for load in loads:
+        load.start()
+
+    barrier = pltpu.get_barrier_semaphore()
+    pl.semaphore_signal(barrier, inc=1, device_id={"tp": other}, device_id_type=MESH)
+    for k in range(1, n):
+        pl.semaphore_signal(
+            barrier, inc=1, device_id={"seq": lax.rem(me + k, n)}, device_id_type=MESH
+        )
+    pl.semaphore_wait(barrier, n)
+
+    def to_peer(source, target, i):
+        return pltpu.make_async_remote_copy(
+            src_ref=source,
+            dst_ref=target,
+            send_sem=pair_send.at[i],
+            recv_sem=pair_recv.at[i],
+            device_id={"tp": other},
+            device_id_type=MESH,
+        )
+
+    def rows_of(index):
+        return pl.ds(pl.multiple_of(index * block, block), block)
+
+    same_head = same_head_ref[...]
+    copies = []
+
+    exchange = to_peer(lat, lat_peer, 0)
+    exchange.start()
+    loads[0].wait()
+    exchange.wait()
+    loads[1].wait()
+    for b in range(batches):
+        rows = jnp.concatenate(
+            [
+                modnorm(lat[b].astype(F32), mod, b, 0).astype(BF16),
+                modnorm(lat_peer[b].astype(F32), mod, b, 0).astype(BF16),
+            ],
+            axis=0,
+        )
+        query, key, value = project(rows, qkv_s, gains, 0, same_head, head_dim)
+        mixed = attend(query, key, value, heads, head_dim, None)
+        part[b] = jnp.dot(mixed, out_s[...], preferred_element_type=F32).astype(BF16)
+        copy = to_peer(part.at[b, pl.ds(patches, patches)], got_s.at[b], 1 + b)
+        copy.start()
+        copies.append(copy)
+    for b in range(batches):
+        copies[b].wait()
+        out = (part[b, :patches].astype(F32) + got_s[b].astype(F32)).astype(BF16).astype(F32)
+        field = lat[b].astype(F32) + mod[b, 2:3, :] * out
+        running[b] = field
+        mixed_f32[:, b] = modnorm(field, mod, b, 3).reshape(n, small, field.shape[-1])
+    send[...] = mixed_f32[...].reshape(send.shape).astype(BF16)
+
+    def swap(source, target, k, sends, receives):
+        to = lax.rem(me + k, n)
+        return pltpu.make_async_remote_copy(
+            src_ref=source.at[rows_of(to)],
+            dst_ref=target.at[rows_of(me)],
+            send_sem=sends.at[k],
+            recv_sem=receives.at[k],
+            device_id={"seq": to},
+            device_id_type=MESH,
+        )
+
+    def landing(target, k, sends, receives):
+        origin = lax.rem(me + n - k, n)
+        return pltpu.make_async_remote_copy(
+            src_ref=target.at[rows_of(origin)],
+            dst_ref=target.at[rows_of(origin)],
+            send_sem=sends.at[k],
+            recv_sem=receives.at[k],
+            device_id={"seq": lax.rem(me + k, n)},
+            device_id_type=MESH,
+        )
+
+    def forward(origin, k):
+        return pltpu.make_async_remote_copy(
+            src_ref=tokens.at[0, rows_of(origin)],
+            dst_ref=tokens.at[1, rows_of(origin)],
+            send_sem=f_send.at[k],
+            recv_sem=f_recv.at[k],
+            device_id={"tp": other},
+            device_id_type=MESH,
+        )
+
+    outgoing = [swap(send, tokens.at[0], k, a_send, a_recv) for k in range(1, n)]
+    for copy in outgoing:
+        copy.start()
+    own = pltpu.make_async_copy(send.at[rows_of(me)], tokens.at[0, rows_of(me)], own_sem.at[0])
+    own.start()
+    own.wait()
+    forwards = [forward(me, 0)]
+    forwards[0].start()
+    for k in range(1, n):
+        landing(tokens.at[0], k, a_send, a_recv).wait_recv()
+        copy = forward(lax.rem(me + n - k, n), k)
+        copy.start()
+        forwards.append(copy)
+    loads[2].wait()
+    loads[3].wait()
+    for copy in forwards:
+        copy.wait()
+    for copy in outgoing:
+        copy.wait_send()
+
+    for chunk in (1, 0):
+        query, key, value = project(tokens[chunk], qkv_t, gains, 2, same_head, head_dim)
+        mixed = attend(query, key, value, heads, head_dim, block)
+        part[chunk] = jnp.dot(mixed, out_t[...], preferred_element_type=F32).astype(BF16)
+        if chunk == 1:
+            share = to_peer(part.at[1], got_t, 1 + batches)
+            share.start()
+    share.wait()
+    back_send[...] = (part[0].astype(F32) + got_t[...].astype(F32)).astype(BF16)
+
+    outgoing = [swap(back_send, back, k, b_send, b_recv) for k in range(1, n)]
+    for copy in outgoing:
+        copy.start()
+    own = pltpu.make_async_copy(back_send.at[rows_of(me)], back.at[rows_of(me)], own_sem.at[1])
+    own.start()
+    own.wait()
+    for k in range(1, n):
+        landing(back, k, b_send, b_recv).wait_recv()
+    for copy in outgoing:
+        copy.wait_send()
+
+    mixed_f32[...] = back[...].astype(F32).reshape(mixed_f32.shape)
+    for b in range(batches):
+        field = running[b] + mod[b, 5:6, :] * mixed_f32[:, b].reshape(running.shape[1:])
+        running[b] = field
+        normed[pl.ds(b * patches, patches)] = modnorm(field, mod, b, 6).astype(BF16)
+    exchange = to_peer(normed, normed_peer, 2 + batches)
+    exchange.start()
+    loads[4].wait()
+    units = w_in.shape[1]
+    tile = next(t for t in (768, 512, 384, 256, 128, units) if units % t == 0)
+
+    def enter(rows, slot):
+        for first in range(0, units, tile):
+            u = jnp.dot(rows, w_in[:, first : first + tile], preferred_element_type=F32)
+            hidden[slot, :, first : first + tile] = gelu(u).astype(BF16)
+
+    enter(normed[...], 0)
+    exchange.wait()
+    enter(normed_peer[...], 1)
+    loads[5].wait()
+    part[1] = jnp.dot(hidden[1], w_out[...], preferred_element_type=F32).astype(BF16)
+    share = to_peer(part.at[1], got_m, 3 + batches)
+    share.start()
+    part[0] = jnp.dot(hidden[0], w_out[...], preferred_element_type=F32).astype(BF16)
+    share.wait()
+    for b in range(batches):
+        rows = pl.ds(b * patches, patches)
+        out = (part[0, rows].astype(F32) + got_m[rows].astype(F32)).astype(BF16).astype(F32)
+        result[b] = (running[b] + mod[b, 8:9, :] * out).astype(BF16)
 
 
 def layer_norm(values):
     average = jnp.mean(values, axis=-1, keepdims=True)
     centred = values - average
     variance = jnp.mean(centred * centred, axis=-1, keepdims=True)
-    return centred * lax.rsqrt(variance + epsilon)
+    return centred * lax.rsqrt(variance + EPSILON)
 
 
 def modulated(field, modulation, offset):
@@ -25,7 +306,7 @@
     return (layer_norm(field) * (1.0 + scale_row) + shift_row).astype(jnp.bfloat16)
 
 
-def project_heads(rows_piece, table, gains, head_dim):
+def project_heads_any(rows_piece, table, gains, head_dim):
     results = []
     for which_part in range(3):
         projected = jnp.einsum(
@@ -37,7 +318,7 @@
             )
             shaped = (
                 shaped
-                * lax.rsqrt(jnp.mean(shaped * shaped, axis=-1, keepdims=True) + epsilon)
+                * lax.rsqrt(jnp.mean(shaped * shaped, axis=-1, keepdims=True) + EPSILON)
                 * gains[which_part]
             )
             projected = shaped.reshape(projected.shape)
@@ -45,7 +326,7 @@
     return jnp.stack(results)
 
 
-def attend(query_rows, key_rows, value_rows, head_dim):
+def attend_any(query_rows, key_rows, value_rows, head_dim):
     groups, length, feature_width = query_rows.shape
     head_count = feature_width // head_dim
     query_heads = query_rows.reshape(groups, length, head_count, head_dim)
@@ -75,11 +356,11 @@
         item.transpose(0, 2, 1, 3).reshape(batches * patches, frames, feature_width)
         for item in (query_rows, key_rows, value_rows)
     ]
-    mixed_heads = attend(members[0], members[1], members[2], head_dim)
+    mixed_heads = attend_any(members[0], members[1], members[2], head_dim)
     return mixed_heads.reshape(batches, patches, frames, feature_width).transpose(0, 2, 1, 3)
 
 
-def body(
+def body_any_width(
     latent,
     modulation,
     qkv_spatial,
@@ -91,14 +372,14 @@
     fc_in,
     fc_out,
 ):
-    head_dim = D // H
+    head_dim = gain_spatial.shape[-1]
     running = latent.astype(jnp.float32)
     normed = modulated(running, modulation, 0)
-    packed = project_heads(
+    packed = project_heads_any(
         lax.all_gather(normed, "tp", axis=2, tiled=True), qkv_spatial, gain_spatial, head_dim
     )
     batches, frames, patches, local_width = packed.shape[1:]
-    mixed_heads = attend(
+    mixed_heads = attend_any(
         packed[0].reshape(batches * frames, patches, local_width),
         packed[1].reshape(batches * frames, patches, local_width),
         packed[2].reshape(batches * frames, patches, local_width),
@@ -114,7 +395,7 @@
     running = running + modulation[:, 2][:, None, None, :] * spatial_out.astype(jnp.float32)
     normed = modulated(running, modulation, 3)
     moved_rows = lax.all_to_all(normed, "seq", split_axis=2, concat_axis=1, tiled=True)
-    packed = project_heads(
+    packed = project_heads_any(
         lax.all_gather(moved_rows, "tp", axis=2, tiled=True), qkv_temporal, gain_temporal, head_dim
     )
     mixed_heads = frame_attention(packed[0], packed[1], packed[2], head_dim)
@@ -143,7 +424,63 @@
     )
 
 
+def body(n, latent, modulation, qkv_s, gain_s, out_s, qkv_t, gain_t, out_t, fc_in, fc_out):
+    batches, frames, patches, width = latent.shape
+    head_dim = gain_s.shape[-1]
+    local = qkv_s.shape[-1]
+    count = batches * patches
+    small = patches // n
+    lane = jnp.arange(local) // head_dim
+    same_head = (lane[:, None] == lane[None, :]).astype(BF16)
+    gains = jnp.tile(jnp.concatenate([gain_s, gain_t], axis=0), (1, local // head_dim))
+    vmem = pl.BlockSpec(memory_space=pltpu.VMEM)
+    hbm = pl.BlockSpec(memory_space=pl.ANY)
+    dma = pltpu.SemaphoreType.DMA
+    weights = (qkv_s, out_s, qkv_t, out_t, fc_in, fc_out)
+    half = (batches, patches, width)
+    flat = (count, width)
+    out = pl.pallas_call(
+        functools.partial(kernel, n, head_dim),
+        out_shape=jax.ShapeDtypeStruct(half, BF16),
+        in_specs=[vmem] * 4 + [hbm] * 6,
+        out_specs=vmem,
+        scratch_shapes=[pltpu.VMEM(w.shape, w.dtype) for w in weights]
+        + [
+            pltpu.VMEM(half, BF16),
+            pltpu.VMEM((2, 2 * patches, width), BF16),
+            pltpu.VMEM(half, BF16),
+            pltpu.VMEM(half, F32),
+            pltpu.VMEM((n, batches, small, width), F32),
+            pltpu.VMEM(flat, BF16),
+            pltpu.VMEM((2,) + flat, BF16),
+            pltpu.VMEM(flat, BF16),
+            pltpu.VMEM(flat, BF16),
+            pltpu.VMEM(flat, BF16),
+            pltpu.VMEM(flat, BF16),
+            pltpu.VMEM(flat, BF16),
+            pltpu.VMEM((2, count, fc_in.shape[1]), BF16),
+            pltpu.VMEM(flat, BF16),
+            pltpu.VMEM((count, local), F32),
+            dma((6,)),
+            dma((4 + batches,)),
+            dma((4 + batches,)),
+            dma((n,)),
+            dma((n,)),
+            dma((n,)),
+            dma((n,)),
+            dma((n,)),
+            dma((n,)),
+            dma((2,)),
+        ],
+        compiler_params=pltpu.CompilerParams(
+            collective_id=0, has_side_effects=True, vmem_limit_bytes=62 * 1024 * 1024
+        ),
+    )(latent.reshape(half), modulation, gains, same_head, *weights)
+    return out.reshape(latent.shape)
+
+
 def solution(mesh):
+    n = mesh.shape["seq"]
     placed = (
         P(None, "seq", "tp", None),
         P(),
@@ -157,5 +494,9 @@
         P("tp", None),
     )
     return jax.shard_map(
-        body, mesh=mesh, in_specs=placed, out_specs=P(None, "seq", "tp", None), check_vma=False
-    )
+        functools.partial(body, n) if mesh.shape["tp"] == 2 else body_any_width,
+        mesh=mesh,
+        in_specs=placed,
+        out_specs=P(None, "seq", "tp", None),
+        check_vma=False,
+    )

time: 190 us -> 83.8 us (0.44)
  Pallas kernels: 0 us -> 64.1 us
  waiting for transfers between devices: 57.6 us -> 0 us
  blocking collectives: 41.8 us -> 0 us
  matrix products: 39.4 us -> 0 us
  other arithmetic: 16.3 us -> 1.86 us
  between operations: 13.8 us -> 0.02 us
    pallas_call x0 -> x1, Pallas kernels: none -> 64.1 us  [body(): pl.pallas_call(functools.partial(kernel, n, head_dim), out_shape=jax.Shap...]
    all_to_all x2 -> x0, blocking collectives: 41.8 us -> none  [the longest x1 20.9 us: body(): lax.all_to_all(normed, 'seq', split_axis=2, concat_axis=1, tiled=True)]
    dot_general x13 -> x0, matrix products: 39.4 us -> none  [the longest x6 18.2 us: project_heads(): jnp.einsum('bfpd,de->bfpe', rows_piece, table[which_part], preferred_elem...]
    all_gather x3 -> x0, waiting for transfers between devices: 28.1 us -> none  [the longest x2 20.9 us: body(): lax.all_gather(normed, 'tp', axis=2, tiled=True)]
    reduce_scatter x2 -> x0, waiting for transfers between devices: 19.6 us -> none  [body(): lax.psum_scatter(partial_value.astype(jnp.bfloat16), 'tp', scatter_dimens...]
    unnamed x23 -> x4, local copies, waits for them, and re-layouts: 2.52 us -> 16.6 us
    unnamed x7 -> x0, waiting for transfers between devices: 9.87 us -> none
    reduce_sum x8 -> x0, other arithmetic: 7.73 us -> none  [the longest x3 3.01 us: layer_norm(): average = jnp.mean(values, axis=-1, keepdims=True)]
  transfers between devices with their start and end apart: 6 -> 0, of which waited for: 6 -> 0; matrix products, arithmetic and copies ran while one was open for 2% -> 0% of each run, Pallas kernels for 0% -> 0%
where the time goes in v1:
time: 83.8 us; the launch traced here: 83.3 us
  Pallas kernels  64.1 us (76%)
  local copies, waits for them, and re-layouts  17.3 us (21%)
  other arithmetic  1.86 us (2%)
    pallas_call x1, Pallas kernels, body(): pl.pallas_call(functools.partial(kernel, n, head_dim), out_shape=jax.Shap...  64.1 us
    unnamed x4, local copies, waits for them, and re-layouts  16.6 us

profile of v1, /device:TPU:29, one launch (start us, length us, event | category | flops | bytes accessed | tf_op | source)
XLA Modules:
  0.0 83.3 jit_solution(9339746485364275329)
XLA Ops:
  0.0 0.7 pad_maximum_fusion
  0.7 0.7 tile.10.gains
  1.4 1.6 %copy.11.mod = f32[2,9,1152]{2,1,0:T(8,128)} copy(f32[2,9,1152]{2,0,1:T(2,128)} %param.11) | data formatting | bytes 165888 | tf_op args[1]
  3.0 1.2 %compare_convert_fusion.same_head_ref = bf16[576,576]{1,0:T(8,128)(2,1)} fusion(s32[576]{0:T(1024)S(1)} %add_select_fusion), kind=kLoop, calls=%fused_computation | loop fusion | flops 663552 | bytes 665856 | tf_op jit(solution)/shard_map/convert_element_type | solution.py:434
  4.1 6.5 %copy.12.h_qkv_s = bf16[3,1152,576]{2,1,0:T(8,128)(2,1)} copy(bf16[3,1152,576]{1,2,0:T(8,128)(2,1)} %param.12) | data formatting | bytes 7962624 | tf_op args[2]
  10.7 6.6 %copy.13.h_qkv_t = bf16[3,1152,576]{2,1,0:T(8,128)(2,1)} copy(bf16[3,1152,576]{1,2,0:T(8,128)(2,1)} %param.15) | data formatting | bytes 7962624 | tf_op args[5]
  17.3 64.1 %shard_map.100 = bf16[2,128,1152]{2,1,0:T(8,128)(2,1)} custom-call(bf16[2,128,1152]{2,1,0:T(8,128)(2,1)} %bitcast.5, f32[2,9,1152]{2,1,0:T(8,128)} %copy.11.mod, f32[4,576]{1,0:T(4,128)} %tile.10.gains, bf16[576,576]{1,0:T(8,128)(2,1)} %compare_convert_fusion.same_head_ref, bf16[3,1152,576]{2,1,0:T(8,128)(2,1)} %copy.12.h_qkv_s, bf16[576,1152]{1,0:T(8,128)(2,1)} %h_out_s.1, ...), custom_call_target="tpu_custom_call" | custom-call | tf_op jit(solution)/shard_map/pallas_call | solution.py:442
  81.4 1.9 %copy.16 = bf16[2,1,128,1152]{3,2,1,0:T(8,128)(2,1)} copy(bf16[2,1,128,1152]{3,2,1,0:T(8,128)(2,1)} %bitcast.4) | data formatting | bytes 1179648
  (2 shorter events, 0.0 us)

commit v2 on v1

--- a/solution.py
+++ b/solution.py
@@ -15,22 +15,24 @@
 
 
 def modnorm(rows, mod_ref, b, offset):
-    shift = mod_ref[b, offset : offset + 1, :]
-    scale = mod_ref[b, offset + 1 : offset + 2, :]
+    shift = mod_ref[offset, b : b + 1, :]
+    scale = mod_ref[offset + 1, b : b + 1, :]
     average = jnp.mean(rows, axis=-1, keepdims=True)
     centred = rows - average
     variance = jnp.mean(centred * centred, axis=-1, keepdims=True)
     return centred * lax.rsqrt(variance + EPSILON) * (1.0 + scale) + shift
 
 
-def project(rows, table_ref, gain_ref, gain_row, same_head, head_dim):
+def project(rows, table_ref, gains, same_head, head_dim):
     results = []
     for part in range(3):
-        y = jnp.dot(rows, table_ref[part], preferred_element_type=F32)
+        y = lax.dot_general(
+            rows, table_ref[part], (((1,), (1,)), ((), ())), preferred_element_type=F32
+        )
         if part < 2:
             squares = jnp.dot((y * y).astype(BF16), same_head, preferred_element_type=F32)
             inverse = lax.rsqrt(squares * (1.0 / head_dim) + EPSILON)
-            y = y * inverse * gain_ref[gain_row + part : gain_row + part + 1, :]
+            y = y * inverse * gains[part : part + 1, :]
         results.append(y.astype(BF16))
     return results
 
@@ -41,7 +43,9 @@
     if group is not None:
         row = lax.broadcasted_iota(jnp.int32, (length, length), 0)
         column = lax.broadcasted_iota(jnp.int32, (length, length), 1)
-        same = lax.rem(row, group) == lax.rem(column, group)
+        same = (lax.rem(row, group) == lax.rem(column, group)) & (
+            (row < length // 2) == (column < length // 2)
+        )
     heads_ref[...] = jnp.zeros_like(heads_ref)
     for head in range(width // head_dim):
         first, last = head * head_dim, (head + 1) * head_dim
@@ -70,13 +74,22 @@
     return 0.5 * u * (1.0 + jnp.tanh(math.sqrt(2.0 / math.pi) * (u + 0.044715 * (u * u * u))))
 
 
+def spread(gain_ref, width):
+    head_dim = gain_ref.shape[-1]
+    row = lax.broadcasted_iota(jnp.int32, (head_dim, width), 0)
+    column = lax.broadcasted_iota(jnp.int32, (head_dim, width), 1)
+    place = jnp.where(lax.rem(column, head_dim) == row, 1.0, 0.0)
+    return jnp.dot(
+        gain_ref[...], place, preferred_element_type=F32, precision=lax.Precision.HIGHEST
+    )
+
+
 def kernel(
     n,
-    head_dim,
     lat,
     mod,
-    gains,
-    same_head_ref,
+    gain_s,
+    gain_t,
     h_qkv_s,
     h_out_s,
     h_qkv_t,
@@ -93,17 +106,16 @@
     lat_peer,
     part,
     got_s,
+    got_t,
+    got_m,
     running,
-    mixed_f32,
     send,
     tokens,
-    got_t,
     back_send,
     back,
     normed,
     normed_peer,
     hidden,
-    got_m,
     heads,
     w_sem,
     pair_send,
@@ -118,9 +130,10 @@
 ):
     me = lax.axis_index("seq")
     other = 1 - lax.axis_index("tp")
-    batches, patches, _ = lat.shape
-    block = batches * patches // n
+    batches, patches, depth = lat.shape
     small = patches // n
+    head_dim = gain_s.shape[-1]
+    width = out_s.shape[0]
 
     loads = [
         pltpu.make_async_copy(source, target, w_sem.at[i])
@@ -135,8 +148,7 @@
             )
         )
     ]
-    for load in loads:
-        load.start()
+    loads[0].start()
 
     barrier = pltpu.get_barrier_semaphore()
     pl.semaphore_signal(barrier, inc=1, device_id={"tp": other}, device_id_type=MESH)
@@ -144,6 +156,11 @@
         pl.semaphore_signal(
             barrier, inc=1, device_id={"seq": lax.rem(me + k, n)}, device_id_type=MESH
         )
+    row_head = lax.div(lax.broadcasted_iota(jnp.int32, (width, 1), 0), head_dim)
+    column_head = lax.div(lax.broadcasted_iota(jnp.int32, (1, width), 1), head_dim)
+    same_head = jnp.where(row_head == column_head, 1.0, 0.0).astype(BF16)
+    gains_s = spread(gain_s, width)
+    gains_t = spread(gain_t, width)
     pl.semaphore_wait(barrier, n)
 
     def to_peer(source, target, i):
@@ -156,17 +173,67 @@
             device_id_type=MESH,
         )
 
-    def rows_of(index):
-        return pl.ds(pl.multiple_of(index * block, block), block)
-
-    same_head = same_head_ref[...]
-    copies = []
+    def swap(source, target, b, k, sends, receives):
+        to = lax.rem(me + k, n)
+        return pltpu.make_async_remote_copy(
+            src_ref=source.at[to, b],
+            dst_ref=target.at[me, b],
+            send_sem=sends.at[b * n + k],
+            recv_sem=receives.at[b * n + k],
+            device_id={"seq": to},
+            device_id_type=MESH,
+        )
+
+    def landing(target, b, k, sends, receives):
+        origin = lax.rem(me + n - k, n)
+        return pltpu.make_async_remote_copy(
+            src_ref=target.at[origin, b],
+            dst_ref=target.at[origin, b],
+            send_sem=sends.at[b * n + k],
+            recv_sem=receives.at[b * n + k],
+            device_id={"seq": lax.rem(me + k, n)},
+            device_id_type=MESH,
+        )
+
+    def forward(source, origin, b, k):
+        return pltpu.make_async_remote_copy(
+            src_ref=source,
+            dst_ref=tokens.at[1, origin, b],
+            send_sem=f_send.at[b * n + k],
+            recv_sem=f_recv.at[b * n + k],
+            device_id={"tp": other},
+            device_id_type=MESH,
+        )
+
+    outgoing = []
 
     exchange = to_peer(lat, lat_peer, 0)
     exchange.start()
     loads[0].wait()
+    for load in loads[1:]:
+        load.start()
     exchange.wait()
-    loads[1].wait()
+    shares = []
+    owns = []
+    forwards = []
+
+    def leave(b):
+        shares[b].wait()
+        out = (part[b, :patches].astype(F32) + got_s[b].astype(F32)).astype(BF16).astype(F32)
+        field = lat[b].astype(F32) + mod[2, b : b + 1, :] * out
+        running[b] = field
+        send[:, b] = modnorm(field, mod, b, 3).reshape(n, small, depth).astype(BF16)
+        for k in range(1, n):
+            copy = swap(send, tokens.at[0], b, k, a_send, a_recv)
+            copy.start()
+            outgoing.append(copy)
+        own = pltpu.make_async_copy(send.at[me, b], tokens.at[0, me, b], own_sem.at[b])
+        own.start()
+        owns.append(own)
+        copy = forward(send.at[me, b], me, b, 0)
+        copy.start()
+        forwards.append([copy])
+
     for b in range(batches):
         rows = jnp.concatenate(
             [
@@ -175,122 +242,86 @@
             ],
             axis=0,
         )
-        query, key, value = project(rows, qkv_s, gains, 0, same_head, head_dim)
+        query, key, value = project(rows, qkv_s, gains_s, same_head, head_dim)
+        if b > 0:
+            leave(b - 1)
+        else:
+            loads[1].wait()
         mixed = attend(query, key, value, heads, head_dim, None)
         part[b] = jnp.dot(mixed, out_s[...], preferred_element_type=F32).astype(BF16)
         copy = to_peer(part.at[b, pl.ds(patches, patches)], got_s.at[b], 1 + b)
         copy.start()
-        copies.append(copy)
-    for b in range(batches):
-        copies[b].wait()
-        out = (part[b, :patches].astype(F32) + got_s[b].astype(F32)).astype(BF16).astype(F32)
-        field = lat[b].astype(F32) + mod[b, 2:3, :] * out
-        running[b] = field
-        mixed_f32[:, b] = modnorm(field, mod, b, 3).reshape(n, small, field.shape[-1])
-    send[...] = mixed_f32[...].reshape(send.shape).astype(BF16)
-
-    def swap(source, target, k, sends, receives):
-        to = lax.rem(me + k, n)
-        return pltpu.make_async_remote_copy(
-            src_ref=source.at[rows_of(to)],
-            dst_ref=target.at[rows_of(me)],
-            send_sem=sends.at[k],
-            recv_sem=receives.at[k],
-            device_id={"seq": to},
-            device_id_type=MESH,
-        )
-
-    def landing(target, k, sends, receives):
-        origin = lax.rem(me + n - k, n)
-        return pltpu.make_async_remote_copy(
-            src_ref=target.at[rows_of(origin)],
-            dst_ref=target.at[rows_of(origin)],
-            send_sem=sends.at[k],
-            recv_sem=receives.at[k],
-            device_id={"seq": lax.rem(me + k, n)},
-            device_id_type=MESH,
-        )
-
-    def forward(origin, k):
-        return pltpu.make_async_remote_copy(
-            src_ref=tokens.at[0, rows_of(origin)],
-            dst_ref=tokens.at[1, rows_of(origin)],
-            send_sem=f_send.at[k],
-            recv_sem=f_recv.at[k],
-            device_id={"tp": other},
-            device_id_type=MESH,
-        )
-
-    outgoing = [swap(send, tokens.at[0], k, a_send, a_recv) for k in range(1, n)]
-    for copy in outgoing:
-        copy.start()
-    own = pltpu.make_async_copy(send.at[rows_of(me)], tokens.at[0, rows_of(me)], own_sem.at[0])
-    own.start()
-    own.wait()
-    forwards = [forward(me, 0)]
-    forwards[0].start()
-    for k in range(1, n):
-        landing(tokens.at[0], k, a_send, a_recv).wait_recv()
-        copy = forward(lax.rem(me + n - k, n), k)
-        copy.start()
-        forwards.append(copy)
+        shares.append(copy)
+    leave(batches - 1)
+
     loads[2].wait()
     loads[3].wait()
-    for copy in forwards:
-        copy.wait()
+    returns = []
+
+    def give_back(b):
+        returns[b].wait()
+        out = (part[b, :patches].astype(F32) + got_t[b].astype(F32)).astype(BF16)
+        back_send[:, b] = out.astype(F32).reshape(n, small, depth).astype(BF16)
+        for k in range(1, n):
+            copy = swap(back_send, back, b, k, b_send, b_recv)
+            copy.start()
+            outgoing.append(copy)
+        own = pltpu.make_async_copy(back_send.at[me, b], back.at[me, b], own_sem.at[batches + b])
+        own.start()
+        owns.append(own)
+
+    for b in range(batches):
+        if b > 0:
+            give_back(b - 1)
+        for k in range(1, n):
+            landing(tokens.at[0], b, k, a_send, a_recv).wait_recv()
+            origin = lax.rem(me + n - k, n)
+            copy = forward(tokens.at[0, origin, b], origin, b, k)
+            copy.start()
+            forwards[b].append(copy)
+        owns[b].wait()
+        for copy in forwards[b]:
+            copy.wait()
+        rows = jnp.concatenate(
+            [tokens[i, :, b].astype(F32).reshape(patches, depth) for i in range(2)], axis=0
+        ).astype(BF16)
+        query, key, value = project(rows, qkv_t, gains_t, same_head, head_dim)
+        mixed = attend(query, key, value, heads, head_dim, small)
+        part[b] = jnp.dot(mixed, out_t[...], preferred_element_type=F32).astype(BF16)
+        copy = to_peer(part.at[b, pl.ds(patches, patches)], got_t.at[b], 1 + batches + b)
+        copy.start()
+        returns.append(copy)
+    give_back(batches - 1)
+
+    loads[4].wait()
+    loads[5].wait()
+    units = w_in.shape[1]
+    tile = next(t for t in (768, 512, 384, 256, 128, units) if units % t == 0)
+    ends = []
+    for b in range(batches):
+        for k in range(1, n):
+            landing(back, b, k, b_send, b_recv).wait_recv()
+        owns[batches + b].wait()
+        field = running[b] + mod[5, b : b + 1, :] * back[:, b].astype(F32).reshape(patches, depth)
+        running[b] = field
+        normed[b] = modnorm(field, mod, b, 6).astype(BF16)
+        exchange = to_peer(normed.at[b], normed_peer.at[b], 1 + 2 * batches + b)
+        exchange.start()
+        exchange.wait()
+        rows = jnp.concatenate([normed[b], normed_peer[b]], axis=0)
+        for first in range(0, units, tile):
+            u = jnp.dot(rows, w_in[:, first : first + tile], preferred_element_type=F32)
+            hidden[:, first : first + tile] = gelu(u).astype(BF16)
+        part[b] = jnp.dot(hidden[...], w_out[...], preferred_element_type=F32).astype(BF16)
+        copy = to_peer(part.at[b, pl.ds(patches, patches)], got_m.at[b], 1 + 3 * batches + b)
+        copy.start()
+        ends.append(copy)
     for copy in outgoing:
         copy.wait_send()
-
-    for chunk in (1, 0):
-        query, key, value = project(tokens[chunk], qkv_t, gains, 2, same_head, head_dim)
-        mixed = attend(query, key, value, heads, head_dim, block)
-        part[chunk] = jnp.dot(mixed, out_t[...], preferred_element_type=F32).astype(BF16)
-        if chunk == 1:
-            share = to_peer(part.at[1], got_t, 1 + batches)
-            share.start()
-    share.wait()
-    back_send[...] = (part[0].astype(F32) + got_t[...].astype(F32)).astype(BF16)
-
-    outgoing = [swap(back_send, back, k, b_send, b_recv) for k in range(1, n)]
-    for copy in outgoing:
-        copy.start()
-    own = pltpu.make_async_copy(back_send.at[rows_of(me)], back.at[rows_of(me)], own_sem.at[1])
-    own.start()
-    own.wait()
-    for k in range(1, n):
-        landing(back, k, b_send, b_recv).wait_recv()
-    for copy in outgoing:
-        copy.wait_send()
-
-    mixed_f32[...] = back[...].astype(F32).reshape(mixed_f32.shape)
     for b in range(batches):
-        field = running[b] + mod[b, 5:6, :] * mixed_f32[:, b].reshape(running.shape[1:])
-        running[b] = field
-        normed[pl.ds(b * patches, patches)] = modnorm(field, mod, b, 6).astype(BF16)
-    exchange = to_peer(normed, normed_peer, 2 + batches)
-    exchange.start()
-    loads[4].wait()
-    units = w_in.shape[1]
-    tile = next(t for t in (768, 512, 384, 256, 128, units) if units % t == 0)
-
-    def enter(rows, slot):
-        for first in range(0, units, tile):
-            u = jnp.dot(rows, w_in[:, first : first + tile], preferred_element_type=F32)
-            hidden[slot, :, first : first + tile] = gelu(u).astype(BF16)
-
-    enter(normed[...], 0)
-    exchange.wait()
-    enter(normed_peer[...], 1)
-    loads[5].wait()
-    part[1] = jnp.dot(hidden[1], w_out[...], preferred_element_type=F32).astype(BF16)
-    share = to_peer(part.at[1], got_m, 3 + batches)
-    share.start()
-    part[0] = jnp.dot(hidden[0], w_out[...], preferred_element_type=F32).astype(BF16)
-    share.wait()
-    for b in range(batches):
-        rows = pl.ds(b * patches, patches)
-        out = (part[0, rows].astype(F32) + got_m[rows].astype(F32)).astype(BF16).astype(F32)
-        result[b] = (running[b] + mod[b, 8:9, :] * out).astype(BF16)
+        ends[b].wait()
+        out = (part[b, :patches].astype(F32) + got_m[b].astype(F32)).astype(BF16).astype(F32)
+        result[b] = (running[b] + mod[8, b : b + 1, :] * out).astype(BF16)
 
 
 def layer_norm(values):
@@ -426,56 +457,46 @@
 
 def body(n, latent, modulation, qkv_s, gain_s, out_s, qkv_t, gain_t, out_t, fc_in, fc_out):
     batches, frames, patches, width = latent.shape
-    head_dim = gain_s.shape[-1]
     local = qkv_s.shape[-1]
-    count = batches * patches
     small = patches // n
-    lane = jnp.arange(local) // head_dim
-    same_head = (lane[:, None] == lane[None, :]).astype(BF16)
-    gains = jnp.tile(jnp.concatenate([gain_s, gain_t], axis=0), (1, local // head_dim))
     vmem = pl.BlockSpec(memory_space=pltpu.VMEM)
     hbm = pl.BlockSpec(memory_space=pl.ANY)
     dma = pltpu.SemaphoreType.DMA
-    weights = (qkv_s, out_s, qkv_t, out_t, fc_in, fc_out)
+    weights = (jnp.swapaxes(qkv_s, 1, 2), out_s, jnp.swapaxes(qkv_t, 1, 2), out_t, fc_in, fc_out)
     half = (batches, patches, width)
-    flat = (count, width)
+    blocks = (n, batches, small, width)
+    pair = 1 + 4 * batches
     out = pl.pallas_call(
-        functools.partial(kernel, n, head_dim),
+        functools.partial(kernel, n),
         out_shape=jax.ShapeDtypeStruct(half, BF16),
         in_specs=[vmem] * 4 + [hbm] * 6,
         out_specs=vmem,
         scratch_shapes=[pltpu.VMEM(w.shape, w.dtype) for w in weights]
         + [
             pltpu.VMEM(half, BF16),
-            pltpu.VMEM((2, 2 * patches, width), BF16),
+            pltpu.VMEM((batches, 2 * patches, width), BF16),
+            pltpu.VMEM(half, BF16),
+            pltpu.VMEM(half, BF16),
             pltpu.VMEM(half, BF16),
             pltpu.VMEM(half, F32),
-            pltpu.VMEM((n, batches, small, width), F32),
-            pltpu.VMEM(flat, BF16),
-            pltpu.VMEM((2,) + flat, BF16),
-            pltpu.VMEM(flat, BF16),
-            pltpu.VMEM(flat, BF16),
-            pltpu.VMEM(flat, BF16),
-            pltpu.VMEM(flat, BF16),
-            pltpu.VMEM(flat, BF16),
-            pltpu.VMEM((2, count, fc_in.shape[1]), BF16),
-            pltpu.VMEM(flat, BF16),
-            pltpu.VMEM((count, local), F32),
+            pltpu.VMEM(blocks, BF16),
+            pltpu.VMEM((2,) + blocks, BF16),
+            pltpu.VMEM(blocks, BF16),
+            pltpu.VMEM(blocks, BF16),
+            pltpu.VMEM(half, BF16),
+            pltpu.VMEM(half, BF16),
+            pltpu.VMEM((2 * patches, fc_in.shape[1]), BF16),
+            pltpu.VMEM((2 * patches, local), F32),
             dma((6,)),
-            dma((4 + batches,)),
-            dma((4 + batches,)),
-            dma((n,)),
-            dma((n,)),
-            dma((n,)),
-            dma((n,)),
-            dma((n,)),
-            dma((n,)),
-            dma((2,)),
-        ],
+            dma((pair,)),
+            dma((pair,)),
+        ]
+        + [dma((batches * n,))] * 6
+        + [dma((2 * batches,))],
         compiler_params=pltpu.CompilerParams(
             collective_id=0, has_side_effects=True, vmem_limit_bytes=62 * 1024 * 1024
         ),
-    )(latent.reshape(half), modulation, gains, same_head, *weights)
+    )(latent.reshape(half), jnp.swapaxes(modulation, 0, 1), gain_s, gain_t, *weights)
     return out.reshape(latent.shape)
 
 

time: 83.8 us -> 59.3 us (0.71)
  local copies, waits for them, and re-layouts: 17.3 us -> 1.92 us
  Pallas kernels: 64.1 us -> 56.9 us
  other arithmetic: 1.86 us -> 0 us
    unnamed x4 -> x1, local copies, waits for them, and re-layouts: 16.6 us -> 1.92 us
    pallas_call x1, Pallas kernels: 64.1 us -> 56.9 us  [body(): pl.pallas_call(functools.partial(kernel, n), out_shape=jax.ShapeDtypeStru...]
    convert_element_type x1 -> x0, other arithmetic: 1.15 us -> none  [body(): same_head = (lane[:, None] == lane[None, :]).astype(BF16)]
where the time goes in v2:
time: 59.3 us; the launch traced here: 58.8 us
  Pallas kernels  56.9 us (96%)
  local copies, waits for them, and re-layouts  1.92 us (3%)
    pallas_call x1, Pallas kernels, body(): pl.pallas_call(functools.partial(kernel, n), out_shape=jax.ShapeDtypeStru...  56.9 us
    unnamed x1, local copies, waits for them, and re-layouts  1.92 us

profile of v2, /device:TPU:29, one launch (start us, length us, event | category | flops | bytes accessed | tf_op | source)
XLA Modules:
  0.0 58.8 jit_solution(7793773632505967667)
XLA Ops:
  0.0 56.9 %shard_map.100 = bf16[2,128,1152]{2,1,0:T(8,128)(2,1)} custom-call(bf16[2,128,1152]{2,1,0:T(8,128)(2,1)} %bitcast.10, f32[9,2,1152]{2,1,0:T(2,128)} %bitcast.11, f32[2,72]{1,0:T(2,128)} %gain_s.1, f32[2,72]{1,0:T(2,128)} %gain_t.1, bf16[3,576,1152]{2,1,0:T(8,128)(2,1)} %bitcast.7, bf16[576,1152]{1,0:T(8,128)(2,1)} %h_out_s.1, bf16[3,576,1152]{2,1,0:T(8,128)(2,1)} %bitcast.8, ...), custom_call_target="tpu_custom_call" | custom-call | tf_op jit(solution)/shard_map/pallas_call | solution.py:469
  56.9 1.9 %copy.13 = bf16[2,1,128,1152]{3,2,1,0:T(8,128)(2,1)} copy(bf16[2,1,128,1152]{3,2,1,0:T(8,128)(2,1)} %bitcast.9) | data formatting | bytes 1179648
